TPU v7x, 32 devices: a whole 2x2x4 slice. The times are simulated.
32 devices in a mesh: section: 4 (over z), expert: 4 (over y, x), dp: 2 (over core).
Axes of the slice: x: 2, y: 2, z: 4, core: 2. Of those that a mesh axis runs over, the one named last changes fastest.
Arguments:
- stash: bfloat16 [4, 256, 2048], P('section', 'dp', 'expert'), may hold values from -6 to 6
- cotangent: bfloat16 [4, 256, 2048], P('section', 'dp', 'expert'), may hold values from -6 to 6
- backward_expert_routes: int32 [4, 256, 2], P('section', 'dp'), may hold values from 0 to 3, all different within a row; in each aligned block of 128 rows (0 to 127, 128 to 255, ..., all dimensions but the last counted through in order) at most 80 rows name the same one
- backward_job_lengths: int32 [4, 4], P('section'), may hold values from 1 to 128, 256 in all within a row
- layer_norm_gains: float32 [4, 2048], P('section'), may hold values from 0.25 to 1.75
- router: bfloat16 [4, 2048, 4], P('section'), may hold values from -0.125 to 0.125
- expert_gate_weight: bfloat16 [4, 2048, 28672], P('section', None, ('expert', 'dp')), may hold values from -0.125 to 0.125
- expert_up_weight: bfloat16 [4, 2048, 28672], P('section', None, ('expert', 'dp')), may hold values from -0.125 to 0.125
- expert_down_weight: bfloat16 [4, 28672, 2048], P('section', ('expert', 'dp')), may hold values from -0.0625 to 0.0625
- adapter_down_maps: bfloat16 [4, 2048, 64], P('section', 'expert'), may hold values from -0.125 to 0.125
- adapter_up_maps: bfloat16 [4, 64, 2048], P('section', None, 'expert'), may hold values from -1.5 to 1.5
Outputs:
- handed_back: bfloat16 [4, 256, 2048], P('section', 'dp', 'expert')
- grad_lora_down: float32 [4, 2048, 64], P('section', 'expert')
- grad_lora_up: float32 [4, 64, 2048], P('section', None, 'expert')
Inputs may be any that keep to these rules, and one draw needn't show every extreme that they name: `backward_expert_routes`: each row names two different experts. In each aligned block of 128 rows (the tokens of one device) no expert is named more than 80 times. `backward_job_lengths`: each row sums to 256.
All inputs are finite; a program needn't handle non-finite values.
Results may differ from a plain program's by a relative error of at most 0.008.
Values may be sent and summed in bfloat16 or wider, within the bound.
A program may use at most 128 MiB of HBM per device.

v0:
```python
import jax
import jax.numpy as jnp
from jax import lax
from jax.sharding import PartitionSpec as P

MODEL_WIDTH = 2048
EXPERTS = 4
ADAPTER_RANK = 16
CAP = 80
EPS = 1e-05
ADAPTER_SCALE = 0.5
HIGH = lax.Precision.HIGHEST


def from_behind(block, axis, distance):
    devices = range(lax.axis_size(axis))
    route = [((i - distance) % len(devices), i) for i in devices]
    return lax.ppermute(block, axis, route)


def job_columns(job_token_lengths, offset, count):
    ends = jnp.cumsum(job_token_lengths, dtype=jnp.int32)
    position = offset + jnp.arange(count, dtype=jnp.int32)
    owner = jnp.sum((ends[None, :] <= position[:, None]).astype(jnp.int32), axis=1, dtype=jnp.int32)
    column_owner = (
        jnp.arange(job_token_lengths.shape[0] * ADAPTER_RANK, dtype=jnp.int32) // ADAPTER_RANK
    )
    return (owner[:, None] == column_owner[None, :]).astype(jnp.float32)


def prepare(whole_batch, norm_gain_vector, router, token_routes):
    expert_values = whole_batch.astype(jnp.float32)
    scale = lax.rsqrt(jnp.mean(expert_values * expert_values, axis=1, keepdims=True) + EPS)
    normalized_input = (expert_values * scale * norm_gain_vector[None, :]).astype(jnp.bfloat16)
    logits = jnp.dot(normalized_input, router, preferred_element_type=jnp.float32)
    labels = jnp.arange(router.shape[1], dtype=jnp.int32)
    first = (token_routes[:, 0:1] == labels[None, :]).astype(jnp.float32)
    second = (token_routes[:, 1:2] == labels[None, :]).astype(jnp.float32)
    upper = jax.nn.sigmoid(jnp.sum(first * logits, axis=1) - jnp.sum(second * logits, axis=1))
    table = upper[:, None] * first + (1.0 - upper)[:, None] * second
    return (expert_values, scale, normalized_input, first, second, upper, table)


def router_grad(gate_grad, first, second, upper):
    spread = jnp.sum(first * gate_grad, axis=1) - jnp.sum(second * gate_grad, axis=1)
    delta = spread * upper * (1.0 - upper)
    return delta[:, None] * (first - second)


def slot_matrix(member, capacity):
    marks = member.astype(jnp.int32)
    ranked = jnp.cumsum(marks, axis=-1, dtype=jnp.int32) - marks
    slots = jnp.arange(capacity, dtype=jnp.int32)
    hit = (ranked[..., None, :] == slots[:, None]) & (marks[..., None, :] == 1)
    return hit.astype(jnp.float32)


def expert_back(
    rows, adapter_gradient_list, expert_gate_weight, expert_up_weight, expert_down_weight
):
    gate = jnp.dot(rows, expert_gate_weight, preferred_element_type=jnp.float32)
    up = jnp.dot(rows, expert_up_weight, preferred_element_type=jnp.float32)
    sig = jax.nn.sigmoid(gate)
    act = gate * sig
    hidden = (act * up).astype(jnp.bfloat16)
    output = jnp.dot(hidden, expert_down_weight, preferred_element_type=jnp.float32)
    gate_term = jnp.sum(adapter_gradient_list.astype(jnp.float32) * output, axis=1)
    back = jnp.dot(adapter_gradient_list, expert_down_weight.T, preferred_element_type=jnp.float32)
    d_gate = (back * up * sig * (1.0 + gate * (1.0 - sig))).astype(jnp.bfloat16)
    d_up = (back * act).astype(jnp.bfloat16)
    d_rows = jnp.dot(d_gate, expert_gate_weight.T, preferred_element_type=jnp.float32) + jnp.dot(
        d_up, expert_up_weight.T, preferred_element_type=jnp.float32
    )
    return (d_rows, gate_term)


def body(
    stash,
    cotangent,
    backward_expert_routes,
    backward_job_lengths,
    layer_norm_gains,
    router,
    expert_gate_weight,
    expert_up_weight,
    expert_down_weight,
    adapter_down_maps,
    adapter_up_maps,
):
    groups = lax.axis_size("expert")
    shards = lax.axis_size("dp")
    column_block = lax.axis_index("expert")
    token_block = lax.axis_index("dp")
    mine = column_block // (groups // EXPERTS)
    s_cols = stash[0]
    gradient_columns = cotangent[0]
    count, width = s_cols.shape
    s_full, g_full = (
        lax.all_gather(s_cols, "expert", axis=1, tiled=True),
        lax.all_gather(gradient_columns, "expert", axis=1, tiled=True),
    )
    norm_gain_vector = layer_norm_gains[0]
    route_w = router[0]
    wg = expert_gate_weight[0]
    wu = expert_up_weight[0]
    wd = expert_down_weight[0]
    down_map_rows = adapter_down_maps[0]
    backward_columns = adapter_up_maps[0]
    col_start = column_block * width
    gain_cols = lax.dynamic_slice_in_dim(norm_gain_vector, col_start, width, 0)
    route_cols = lax.dynamic_slice_in_dim(route_w, col_start, width, 0)
    offset = token_block * count
    backward_mask = job_columns(backward_job_lengths[0], offset, count)
    b_values, b_scale, b_normed, b_first, b_second, b_upper, b_table = prepare(
        s_full, norm_gain_vector, route_w, backward_expert_routes[0]
    )
    labels = jnp.arange(EXPERTS, dtype=jnp.int32)
    own = (labels == mine).astype(jnp.float32)
    b_member = jnp.sum((b_first + b_second) * own[None, :], axis=1)
    b_gate = jnp.sum(b_table * own[None, :], axis=1)
    b_slots = slot_matrix(b_member, CAP)
    b_normed_cols = lax.dynamic_slice_in_dim(b_normed, col_start, width, 1)
    a_full = lax.all_gather(down_map_rows, "expert", axis=0, tiled=True)
    b_low = jnp.dot(b_normed, a_full, preferred_element_type=jnp.float32)
    grad_low_rank = lax.psum(
        jnp.dot(gradient_columns, backward_columns.T, preferred_element_type=jnp.float32), "expert"
    )
    backward_low_rank = (b_low * backward_mask).astype(jnp.bfloat16)
    grad_low_rank_backward = (ADAPTER_SCALE * grad_low_rank * backward_mask).astype(jnp.bfloat16)
    up_map_gradient = ADAPTER_SCALE * jnp.dot(
        backward_low_rank.T, gradient_columns, preferred_element_type=jnp.float32
    )
    down_map_gradient = jnp.dot(
        b_normed_cols.T, grad_low_rank_backward, preferred_element_type=jnp.float32
    )
    down_map_gradient, up_map_gradient = lax.psum((down_map_gradient, up_map_gradient), "dp")
    normalized_grad_adapter = jnp.dot(
        grad_low_rank_backward, down_map_rows.T, preferred_element_type=jnp.float32
    )
    b_slots_low = b_slots.astype(jnp.bfloat16)
    b_sel = jnp.dot(b_slots_low, b_normed, preferred_element_type=jnp.float32).astype(jnp.bfloat16)
    g_sel = jnp.dot(b_slots_low, g_full, preferred_element_type=jnp.float32).astype(jnp.bfloat16)
    b_rows, g_rows = (
        lax.all_gather(b_sel, "dp", axis=0, tiled=True),
        lax.all_gather(g_sel, "dp", axis=0, tiled=True),
    )
    dn_slots, dgam_slots = expert_back(b_rows, g_rows, wg, wu, wd)
    b_member_all, b_gate_all = (
        lax.all_gather(b_member, "dp", axis=0, tiled=True),
        lax.all_gather(b_gate, "dp", axis=0, tiled=True),
    )
    b_all = slot_matrix(b_member_all.reshape(shards, count), CAP)
    b_terms = jnp.einsum(
        "pct,pcex->eptx", b_all, dn_slots.reshape(shards, CAP, groups, width), precision=HIGH
    )
    b_terms = b_terms * b_gate_all.reshape(shards, count)[None, :, :, None]
    normalized_grad_experts = lax.psum_scatter(
        b_terms.reshape(groups * shards * count, width),
        ("expert", "dp"),
        scatter_dimension=0,
        tiled=True,
    )
    dgam_own = lax.psum_scatter(dgam_slots, "dp", scatter_dimension=0, tiled=True)
    dgam_tokens = jnp.dot(dgam_own, b_slots, precision=HIGH)
    gate_part = dgam_tokens[:, None] * own[None, :]
    expert_base_output = normalized_grad_experts + normalized_grad_adapter
    b_values_cols = lax.dynamic_slice_in_dim(b_values, col_start, width, 1)
    route_cols_t = route_cols.astype(jnp.float32).T
    base_weighted = expert_base_output * gain_cols[None, :]
    stat_part = jnp.sum(base_weighted * b_values_cols, axis=1, keepdims=True)
    gate_grad, stat_part = lax.psum((gate_part, stat_part), "expert")
    d_logit = router_grad(gate_grad, b_first, b_second, b_upper)
    lifted = jnp.dot(
        b_values * norm_gain_vector[None, :], route_w.astype(jnp.float32), precision=HIGH
    )
    stat = stat_part + jnp.sum(d_logit * lifted, axis=1, keepdims=True)
    weighted = base_weighted + jnp.dot(d_logit, route_cols_t, precision=HIGH) * gain_cols[None, :]
    layer_result = (
        gradient_columns.astype(jnp.float32)
        + b_scale * weighted
        - b_values_cols * b_scale * b_scale * b_scale * stat / MODEL_WIDTH
    )
    handed_back = from_behind(layer_result.astype(jnp.bfloat16), "section", -1)
    return (handed_back[None], down_map_gradient[None], up_map_gradient[None])


def solution(mesh):
    return jax.shard_map(
        body,
        mesh=mesh,
        in_specs=(
            P("section", "dp", "expert"),
            P("section", "dp", "expert"),
            P("section", "dp", None),
            P("section", None),
            P("section", None),
            P("section", None, None),
            P("section", None, ("expert", "dp")),
            P("section", None, ("expert", "dp")),
            P("section", ("expert", "dp"), None),
            P("section", "expert", None),
            P("section", None, "expert"),
        ),
        out_specs=(
            P("section", "dp", "expert"),
            P("section", "expert", None),
            P("section", None, "expert"),
        ),
        check_vma=False,
    )
```

profile of v0, /device:TPU:0, one launch (start us, length us, event | category | flops | bytes accessed | tf_op | source)
XLA Modules:
  0.0 168.8 jit_solution(5793704472606777799)
XLA Ops:
  8.0 0.0 copy-start
  8.0 0.0 copy-start.2
  8.0 0.0 reduce-scatter.2.cloned.1.call-start
  8.1 12.0 %all-gather = bf16[1,128,2048]{2,1,0:T(8,128)(2,1)S(1)} all-gather(bf16[1,128,512]{2,1,0:T(8,128)(2,1)} %param.11), channel_id=2, replica_groups=mesh['section'=4,'expert'=4,'dp'=2] {'expert'}, dimensions={2}, use_global_device_ids=true | all-gather | bytes 655360 | tf_op jit(solution)/shard_map/all_gather | solution.py:99
  20.1 0.2 fusion.33
  20.3 0.8 slice_bitcast_fusion.1
  21.0 0.9 fusion.35
  21.9 1.0 select_reduce_fusion.2
  22.9 0.1 multiply_reduce_fusion
  23.0 1.8 %all-gather.3 = f32[2,1,128]{2,1,0:T(1,128)S(1)} all-gather(f32[1,1,128]{2,1,0:T(1,128)S(1)} %bitcast.144), channel_id=1, replica_groups=mesh['section'=4,'expert'=4,'dp'=2] {'dp'}, dimensions={0}, use_global_device_ids=true | all-gather | bytes 1536 | tf_op jit(solution)/shard_map/all_gather | solution.py:149
  24.9 0.1 copy.25
  25.0 0.2 reduce-window.16
  25.1 0.1 reduce
  25.3 0.0 copy-done.2
  25.3 9.7 %all-gather.1 = bf16[1,128,2048]{2,1,0:T(8,128)(2,1)S(1)} all-gather(bf16[1,128,512]{2,1,0:T(8,128)(2,1)S(1)} %copy-done.2), channel_id=3, replica_groups=mesh['section'=4,'expert'=4,'dp'=2] {'expert'}, dimensions={2}, use_global_device_ids=true | all-gather | bytes 655360 | tf_op jit(solution)/shard_map/all_gather | solution.py:100
  34.9 0.2 convolution_convert_fusion
  35.2 0.2 convolution_convert_fusion.1
  35.4 2.3 %all_gather.23 = bf16[160,2048]{1,0:T(8,128)(2,1)S(1)} all-gather(bf16[80,2048]{1,0:T(8,128)(2,1)S(1)} %convolution_convert_fusion.1), channel_id=1, replica_groups=mesh['section'=4,'expert'=4,'dp'=2] {'dp'}, dimensions={0}, use_global_device_ids=true | all-gather | bytes 983040 | tf_op jit(solution)/shard_map/all_gather | solution.py:145
  37.7 2.3 %all_gather.24 = bf16[160,2048]{1,0:T(8,128)(2,1)S(1)} all-gather(bf16[80,2048]{1,0:T(8,128)(2,1)S(1)} %convolution_convert_fusion), channel_id=1, replica_groups=mesh['section'=4,'expert'=4,'dp'=2] {'dp'}, dimensions={0}, use_global_device_ids=true | all-gather | bytes 983040 | tf_op jit(solution)/shard_map/all_gather | solution.py:144
  40.0 9.3 %fusion.2 = f32[160,3584]{1,0:T(8,128)} fusion(bf16[160,2048]{1,0:T(8,128)(2,1)S(1)} %all_gather.24, bf16[1,2048,3584]{2,1,0:T(8,128)(2,1)} %param.17), kind=kOutput, calls=%fused_computation.2 | convolution fusion | flops 2348810240 | bytes 17629184 | tf_op jit(solution)/shard_map/dot_general | solution.py:61
  49.3 0.9 copy-done.1
  50.1 3.9 %fusion.6 = f32[160,3584]{1,0:T(8,128)} fusion(bf16[160,2048]{1,0:T(8,128)(2,1)S(1)} %all_gather.24, bf16[1,2048,3584]{2,1,0:T(8,128)(2,1)S(1)} %copy-done.1), kind=kOutput, calls=%fused_computation.6 | convolution fusion | flops 2348810240 | bytes 17629184 | tf_op jit(solution)/shard_map/dot_general | solution.py:62
  54.1 11.6 %fusion.10 = f32[160,3584]{1,0:T(8,128)} fusion(bf16[160,2048]{1,0:T(8,128)(2,1)S(1)} %all_gather.23, bf16[1,3584,2048]{2,1,0:T(8,128)(2,1)} %param.19), kind=kOutput, calls=%fused_computation.10 | convolution fusion | flops 2348810240 | bytes 17629184 | tf_op jit(solution)/shard_map/dot_general | solution.py:68
  65.7 12.1 %fusion = f32[160,2048]{1,0:T(8,128)S(1)} fusion(bf16[1,2048,3584]{2,1,0:T(8,128)(2,1)} %param.17, f32[160,3584]{1,0:T(8,128)} %fusion.2, f32[160,3584]{1,0:T(8,128)} %fusion.10, f32[160,3584]{1,0:T(8,128)} %fusion.6), kind=kOutput, calls=%fused_computation | convolution fusion | flops 2354544640 | bytes 22872064 | tf_op jit(solution)/shard_map/dot_general | solution.py:71
  77.8 12.7 %fusion.15 = f32[160,2048]{1,0:T(8,128)} fusion(f32[160,2048]{1,0:T(8,128)S(1)} %fusion, bf16[1,2048,3584]{2,1,0:T(8,128)(2,1)} %param.18, f32[160,3584]{1,0:T(8,128)} %fusion.10, f32[160,3584]{1,0:T(8,128)} %fusion.2), kind=kOutput, calls=%fused_computation.13 | convolution fusion | flops 2352578560 | bytes 21889024 | tf_op jit(solution)/shard_map/dot_general | solution.py:71
  90.5 2.2 %reshape.159 = f32[2,80,4,512]{3,2,1,0:T(4,128)S(1)} reshape(f32[160,2048]{1,0:T(8,128)} %fusion.15) | data formatting | bytes 2621440 | tf_op jit(solution)/shard_map/reshape | solution.py:154
  92.7 0.3 reduce_window_sum.25
  93.0 1.8 %all-gather.4 = f32[2,1,128]{2,1,0:T(1,128)S(1)} all-gather(f32[1,1,128]{2,1,0:T(1,128)S(1)} %bitcast.143), channel_id=1, replica_groups=mesh['section'=4,'expert'=4,'dp'=2] {'dp'}, dimensions={0}, use_global_device_ids=true | all-gather | bytes 1536 | tf_op jit(solution)/shard_map/all_gather | solution.py:150
  94.8 1.5 multiply_bitcast_fusion
  96.4 0.0 copy-start.6
  96.4 0.0 copy-start.3
  96.4 1.6 copy.28
  98.0 0.0 reduce-scatter.2.cloned.1.call-update
  98.0 0.0 all-reduce.5.cloned.1.call-start
  98.1 0.0 copy-done.6
  98.1 0.2 reduce-window.17
  98.2 0.0 copy-done
  98.3 0.2 fusion.48
  98.4 15.4 %psum.35 = f32[128,64]{0,1:T(8,128)S(1)} all-reduce(f32[128,64]{0,1:T(8,128)S(1)} %fusion.48), channel_id=1, replica_groups=mesh['section'=4,'expert'=4,'dp'=2] {'expert'}, use_global_device_ids=true, to_apply=%region_10.11 | all-reduce | flops 8192 | bytes 65536 | tf_op jit(solution)/shard_map/psum | solution.py:125
  113.8 0.0 copy-done.3
  113.8 9.4 %all-gather.2 = bf16[1,2048,64]{1,2,0:T(8,128)(2,1)S(1)} all-gather(bf16[1,512,64]{1,2,0:T(8,128)(2,1)S(1)} %copy-done.3), channel_id=4, replica_groups=mesh['section'=4,'expert'=4,'dp'=2] {'expert'}, dimensions={1}, use_global_device_ids=true | all-gather | bytes 327680 | tf_op jit(solution)/shard_map/all_gather | solution.py:123
  123.2 0.1 convert_reduce_fusion
  123.3 0.9 convolution_bitcast_fusion
  124.2 1.1 fusion.30
  125.3 0.0 all-reduce.5.cloned.1.call-update
  125.3 0.0 copy-start.5
  125.3 0.0 copy-start.7
  125.3 9.5 %fusion.20 = f32[160]{0:T(256)S(1)} fusion(bf16[1,3584,2048]{2,1,0:T(8,128)(2,1)} %param.19, bf16[160,2048]{1,0:T(8,128)(2,1)S(1)} %all_gather.23, f32[160,3584]{1,0:T(8,128)} %fusion.6, f32[160,3584]{1,0:T(8,128)} %fusion.2), kind=kOutput, calls=%fused_computation.23 | convolution fusion | flops 2353233664 | bytes 19923584 | tf_op jit(solution)/shard_map/dot_general | solution.py:66
  134.9 0.0 copy-start.4
  134.9 0.1 convert_element_type.123
  135.0 2.5 %all-reduce = f32[160]{0:T(256)S(1)} all-reduce(f32[160]{0:T(256)S(1)} %fusion.20), channel_id=6, replica_groups=mesh['section'=4,'expert'=4,'dp'=2] {'dp'}, use_global_device_ids=true, to_apply=%region_12.13.clone | all-reduce | flops 160 | bytes 1280
  137.5 0.6 dynamic-slice.3
  138.7 0.2 convolution_bitcast_fusion.1
  138.9 0.1 broadcast_multiply_fusion
  139.0 1.3 reduce-scatter.2.cloned.1.call-done
  140.3 1.3 fusion.47
  141.6 8.9 %all-reduce.1 = (f32[128,1]{0,1:T(1,128)S(1)}, f32[128,4]{0,1:T(4,128)S(1)}) all-reduce(f32[128,1]{0,1:T(1,128)S(1)} %bitcast.140, f32[128,4]{0,1:T(4,128)S(1)} %broadcast_multiply_fusion), channel_id=1, replica_groups=mesh['section'=4,'expert'=4,'dp'=2] {'expert'}, use_global_device_ids=true, to_apply=%region_17.18 | all-reduce | flops 640 | bytes 5120 | tf_op jit(solution)/shard_map/psum | solution.py:171
  150.6 0.7 fusion.32
  151.3 0.4 fusion.28
  151.6 3.4 %collective-permute-start = (bf16[128,512]{1,0:T(8,128)(2,1)S(1)}, bf16[128,512]{1,0:T(8,128)(2,1)S(1)}, u32[]{:S(2)}, u32[]{:S(2)}) collective-permute-start(bf16[128,512]{1,0:T(8,128)(2,1)S(1)} %fusion.28), channel_id=1, source_target_pairs={{8,0},{16,8},{24,16},{0,24},{9,1},{17,9},{25,17},{1,25},{10,2},{18... | collective-permute-start | bytes 393224 | tf_op jit(solution)/shard_map/ppermute | solution.py:18
  155.1 2.5 %collective-permute-done = bf16[128,512]{1,0:T(8,128)(2,1)S(1)} collective-permute-done((bf16[128,512]{1,0:T(8,128)(2,1)S(1)}, bf16[128,512]{1,0:T(8,128)(2,1)S(1)}, u32[]{:S(2)}, u32[]{:S(2)}) %collective-permute-start) | collective-permute-done | bytes 131104 | tf_op jit(solution)/shard_map/ppermute | solution.py:18
  157.6 0.7 copy.35
  158.2 1.6 copy.36
  159.8 1.6 copy.37
  (20 shorter events, 0.1 us)
Async XLA Ops:
  8.0 90.3 %copy-start = (bf16[1,64,512]{2,1,0:T(8,128)(2,1)S(1)}, bf16[1,64,512]{2,1,0:T(8,128)(2,1)}, u32[]{:S(2)}) copy-start(bf16[1,64,512]{2,1,0:T(8,128)(2,1)} %param.21) | copy-start | bytes 196612
  8.0 17.2 %copy-start.2 = (bf16[1,128,512]{2,1,0:T(8,128)(2,1)S(1)}, bf16[1,128,512]{2,1,0:T(8,128)(2,1)}, u32[]{:S(2)}) copy-start(bf16[1,128,512]{2,1,0:T(8,128)(2,1)} %param.12) | copy-start | bytes 393220
  8.0 132.3 %reduce-scatter.2.cloned.1.call-start = ((), (), s32[]{:S(2)}) async-start(), calls=%async_computation.1 | async-start | bytes 2359296 | tf_op jit(solution)/shard_map/reduce_scatter | solution.py:157
  40.0 10.2 %copy-start.1 = (bf16[1,2048,3584]{2,1,0:T(8,128)(2,1)S(1)}, bf16[1,2048,3584]{2,1,0:T(8,128)(2,1)}, u32[]{:S(2)}) copy-start(bf16[1,2048,3584]{2,1,0:T(8,128)(2,1)} %param.18) | copy-start | bytes 44040196
  96.4 1.7 %copy-start.6 = (s32[1,4]{1,0:T(1,128)S(1)}, s32[1,4]{1,0:T(1,128)}, u32[]{:S(2)}) copy-start(s32[1,4]{1,0:T(1,128)} %param.14) | copy-start | bytes 52
  96.4 17.4 %copy-start.3 = (bf16[1,512,64]{1,2,0:T(8,128)(2,1)S(1)}, bf16[1,512,64]{1,2,0:T(8,128)(2,1)}, u32[]{:S(2)}) copy-start(bf16[1,512,64]{1,2,0:T(8,128)(2,1)} %param.20) | copy-start | bytes 196612
  98.0 59.6 %all-reduce.5.cloned.1.call-start = ((), (), s32[]{:S(2)}) async-start(), calls=%async_computation.2 | async-start | bytes 524288 | tf_op jit(solution)/shard_map/psum | solution.py:136
  125.3 9.6 %copy-start.5 = (f32[1,2048]{1,0:T(1,128)S(1)}, f32[1,2048]{1,0:T(1,128)}, u32[]{:S(2)}) copy-start(f32[1,2048]{1,0:T(1,128)} %param.15) | copy-start | bytes 24580
  125.3 12.2 %copy-start.7 = (u32[32]{0:T(128)S(1)}, u32[32]{0:T(128)}, u32[]{:S(2)}) copy-start(u32[32]{0:T(128)} %constant.94) | copy-start | bytes 388
  134.9 15.7 %copy-start.4 = (bf16[1,2048,4]{1,2,0:T(4,128)(2,1)S(1)}, bf16[1,2048,4]{1,2,0:T(4,128)(2,1)}, u32[]{:S(2)}) copy-start(bf16[1,2048,4]{1,2,0:T(4,128)(2,1)} %param.16) | copy-start | bytes 49156
  151.6 6.0 %collective-permute-start = (bf16[128,512]{1,0:T(8,128)(2,1)S(1)}, bf16[128,512]{1,0:T(8,128)(2,1)S(1)}, u32[]{:S(2)}, u32[]{:S(2)}) collective-permute-start(bf16[128,512]{1,0:T(8,128)(2,1)S(1)} %fusion.28), channel_id=1, source_target_pairs={{8,0},{16,8},{24,16},{0,24},{9,1},{17,9},{25,17},{1,25},{10,2},{18... | collective-permute-start | bytes 393224 | tf_op jit(solution)/shard_map/ppermute | solution.py:18
Sparse Core Ops, SparseCore 0:
  98.1 42.1 reduce-scatter.1
Sparse Core Ops, SparseCore 1:
  125.4 18.3 all-reduce.4
where the time goes:
time: 169 us
  matrix products  66.8 us (40%)
  blocking collectives  66 us (39%)
  between operations  16.4 us (10%)
  local copies, waits for them, and re-layouts  9.96 us (6%)
  waiting for transfers between devices  3.87 us (2%)
  starting transfers between devices  3.51 us (2%)
  other arithmetic  2.28 us (1%)
    psum x1, blocking collectives, body(): lax.psum(jnp.dot(gradient_columns, backward_columns.T, preferred_element_...  15.4 us
    dot_general x1, matrix products, expert_back(): jnp.dot(d_up, expert_up_weight.T, preferred_element_type=jnp.float32)  12.7 us
    dot_general x1, matrix products, expert_back(): jnp.dot(d_gate, expert_gate_weight.T, preferred_element_type=jnp.float32)  12.1 us
    all_gather x1, blocking collectives, body(): lax.all_gather(s_cols, 'expert', axis=1, tiled=True)  12 us
    dot_general x1, matrix products, expert_back(): jnp.dot(adapter_gradient_list, expert_down_weight.T, preferred_element_ty...  11.6 us
    all_gather x1, blocking collectives, body(): lax.all_gather(gradient_columns, 'expert', axis=1, tiled=True)  9.67 us
    dot_general x1, matrix products, expert_back(): jnp.dot(hidden, expert_down_weight, preferred_element_type=jnp.float32)  9.53 us
    all_gather x1, blocking collectives, body(): a_full = lax.all_gather(down_map_rows, 'expert', axis=0, tiled=True)  9.38 us
  transfers between devices with their start and end apart: 3, of which 2 were waited for; matrix products, arithmetic and copies ran while one was open for 9% of the time, Pallas kernels for 0%

commit v1 on v0

--- a/solution.py
+++ b/solution.py
@@ -10,6 +10,13 @@
 EPS = 1e-05
 ADAPTER_SCALE = 0.5
 HIGH = lax.Precision.HIGHEST
+
+
+def link_weights(matrix):
+    parts_seen = []
+    for _ in range(lax.axis_size("expert")):
+        parts_seen.append(matrix)
+    return jnp.concatenate(lax.all_to_all(jnp.stack(parts_seen, 0), "expert", 0, 0), 1)
 
 
 def from_behind(block, axis, distance):
@@ -96,7 +103,7 @@
     gradient_columns = cotangent[0]
     count, width = s_cols.shape
     s_full, g_full = (
-        lax.all_gather(s_cols, "expert", axis=1, tiled=True),
+        link_weights(s_cols),
         lax.all_gather(gradient_columns, "expert", axis=1, tiled=True),
     )
     norm_gain_vector = layer_norm_gains[0]

time: 169 us -> 176 us (1.041)
  blocking collectives: 66 us -> 57.7 us
  starting transfers between devices: 3.51 us -> 8.96 us
  other arithmetic: 2.28 us -> 7.15 us
  local copies, waits for them, and re-layouts: 9.96 us -> 13.4 us
    all_gather x1 -> x0, blocking collectives: 12 us -> none  [body(): lax.all_gather(s_cols, 'expert', axis=1, tiled=True)]
    all_to_all x0 -> x1, starting transfers between devices: none -> 5.19 us  [link_weights(): lax.all_to_all(jnp.stack(parts_seen, 0), 'expert', 0, 0)]
    convert_element_type x0 -> x1, local copies, waits for them, and re-layouts: none -> 2.52 us  [prepare(): expert_values = whole_batch.astype(jnp.float32)]
    all_gather x1, blocking collectives: 9.67 us -> 12.2 us  [body(): lax.all_gather(gradient_columns, 'expert', axis=1, tiled=True)]
    another operation x0 -> x1, local copies, waits for them, and re-layouts: none -> 1.77 us  [link_weights(): jnp.stack(parts_seen, 0)]
    unnamed x20 -> x41, local copies, waits for them, and re-layouts: 5.31 us -> 4.97 us
  transfers between devices with their start and end apart: 3 -> 4, of which waited for: 2 -> 2; matrix products, arithmetic and copies ran while one was open for 9% -> 11% of each run, Pallas kernels for 0% -> 0%
where the time goes in v1:
time: 176 us; the launch traced here: 175 us
  matrix products  68.1 us (39%)
  blocking collectives  57.7 us (33%)
  between operations  16.5 us (9%)
  local copies, waits for them, and re-layouts  13.4 us (8%)
  starting transfers between devices  8.96 us (5%)
  other arithmetic  7.15 us (4%)
  waiting for transfers between devices  3.51 us (2%)
    psum x1, blocking collectives, body(): lax.psum(jnp.dot(gradient_columns, backward_columns.T, preferred_element_...  15.3 us
    dot_general x1, matrix products, expert_back(): jnp.dot(d_up, expert_up_weight.T, preferred_element_type=jnp.float32)  12.8 us
    all_gather x1, blocking collectives, body(): lax.all_gather(gradient_columns, 'expert', axis=1, tiled=True)  12.2 us
    dot_general x1, matrix products, expert_back(): jnp.dot(d_gate, expert_gate_weight.T, preferred_element_type=jnp.float32)  12.1 us
    dot_general x1, matrix products, expert_back(): jnp.dot(adapter_gradient_list, expert_down_weight.T, preferred_element_ty...  11.6 us
    all_gather x1, blocking collectives, body(): a_full = lax.all_gather(down_map_rows, 'expert', axis=0, tiled=True)  10.2 us
    dot_general x1, matrix products, expert_back(): jnp.dot(hidden, expert_down_weight, preferred_element_type=jnp.float32)  10.1 us
    dot_general x1, matrix products, expert_back(): gate = jnp.dot(rows, expert_gate_weight, preferred_element_type=jnp.float32)  9.28 us
  transfers between devices with their start and end apart: 4, of which 2 were waited for; matrix products, arithmetic and copies ran while one was open for 11% of the time, Pallas kernels for 0%

profile of v1, /device:TPU:0, one launch (start us, length us, event | category | flops | bytes accessed | tf_op | source)
XLA Modules:
  0.0 175.3 jit_solution(2333270980339822736)
XLA Ops:
  8.0 0.0 copy-start
  8.0 1.8 %stack.3 = bf16[4,128,512]{2,1,0:T(8,128)(2,1)} broadcast(bf16[128,512]{1,0:T(8,128)(2,1)} %bitcast.122), dimensions={1,2} | broadcast | bytes 655360 | tf_op jit(solution)/shard_map/stack | solution.py:19
  9.8 5.2 %all-to-all-start = ((bf16[4,128,512]{2,1,0:T(8,128)(2,1)}), bf16[4,128,512]{2,1,0:T(8,128)(2,1)S(1)}, u32[]{:S(2)}, u32[]{:S(2)}) async-start(bf16[4,128,512]{2,1,0:T(8,128)(2,1)} %stack.3), calls=%async_computation | async-start | bytes 1048576 | tf_op jit(solution)/shard_map/all_to_all | solution.py:19
  15.0 0.5 broadcast.159
  15.5 1.4 reduce.6
  16.9 12.2 %all-gather = bf16[1,128,2048]{2,1,0:T(8,128)(2,1)S(1)} all-gather(bf16[1,128,512]{2,1,0:T(8,128)(2,1)} %param.12), channel_id=2, replica_groups=mesh['section'=4,'expert'=4,'dp'=2] {'expert'}, dimensions={2}, use_global_device_ids=true | all-gather | bytes 655360 | tf_op jit(solution)/shard_map/all_gather | solution.py:107
  29.1 0.3 copy.32
  29.4 0.0 copy-start.5
  29.4 0.3 multiply_reduce_fusion
  29.7 1.1 convert_element_type.117
  30.7 1.4 convert_multiply_fusion
  32.1 0.2 select_reduce_fusion.2
  32.3 0.1 multiply_reduce_fusion.2
  32.4 1.8 %all-gather.2 = f32[2,1,128]{2,1,0:T(1,128)S(1)} all-gather(f32[1,1,128]{2,1,0:T(1,128)S(1)} %bitcast.133), channel_id=1, replica_groups=mesh['section'=4,'expert'=4,'dp'=2] {'dp'}, dimensions={0}, use_global_device_ids=true | all-gather | bytes 1536 | tf_op jit(solution)/shard_map/all_gather | solution.py:156
  34.3 2.5 %copy.39 = f32[128,2048]{1,0:T(8,128)} copy(f32[128,2048]{0,1:T(8,128)} %bitcast.120) | data formatting | bytes 2097152 | tf_op jit(solution)/shard_map/convert_element_type | solution.py:39
  36.8 1.8 %all-gather.3 = f32[2,1,128]{2,1,0:T(1,128)S(1)} all-gather(f32[1,1,128]{2,1,0:T(1,128)S(1)} %bitcast.134), channel_id=1, replica_groups=mesh['section'=4,'expert'=4,'dp'=2] {'dp'}, dimensions={0}, use_global_device_ids=true | all-gather | bytes 1536 | tf_op jit(solution)/shard_map/all_gather | solution.py:157
  38.6 0.3 reduce_window_sum.25
  38.9 0.1 copy.33
  39.0 0.2 reduce-window.16
  39.2 0.1 reduce.2
  39.3 1.4 multiply_convert_fusion.7
  40.7 0.2 convolution_convert_fusion
  41.0 0.0 slice-start.1
  41.0 0.2 convolution_convert_fusion.1
  41.2 2.4 %all_gather.19 = bf16[160,2048]{1,0:T(8,128)(2,1)S(1)} all-gather(bf16[80,2048]{1,0:T(8,128)(2,1)S(1)} %convolution_convert_fusion.1), channel_id=1, replica_groups=mesh['section'=4,'expert'=4,'dp'=2] {'dp'}, dimensions={0}, use_global_device_ids=true | all-gather | bytes 983040 | tf_op jit(solution)/shard_map/all_gather | solution.py:152
  43.6 2.4 %all_gather.20 = bf16[160,2048]{1,0:T(8,128)(2,1)S(1)} all-gather(bf16[80,2048]{1,0:T(8,128)(2,1)S(1)} %convolution_convert_fusion), channel_id=1, replica_groups=mesh['section'=4,'expert'=4,'dp'=2] {'dp'}, dimensions={0}, use_global_device_ids=true | all-gather | bytes 983040 | tf_op jit(solution)/shard_map/all_gather | solution.py:151
  46.1 9.3 %fusion.2 = f32[160,3584]{1,0:T(8,128)} fusion(bf16[160,2048]{1,0:T(8,128)(2,1)S(1)} %all_gather.20, bf16[1,2048,3584]{2,1,0:T(8,128)(2,1)} %param.17), kind=kOutput, calls=%fused_computation.2 | convolution fusion | flops 2348810240 | bytes 17629184 | tf_op jit(solution)/shard_map/dot_general | solution.py:68
  55.4 3.9 %fusion.6 = f32[160,3584]{1,0:T(8,128)} fusion(bf16[160,2048]{1,0:T(8,128)(2,1)S(1)} %all_gather.20, bf16[1,2048,3584]{2,1,0:T(8,128)(2,1)S(1)} %bitcast.117), kind=kOutput, calls=%fused_computation.6 | convolution fusion | flops 2348810240 | bytes 17629184 | tf_op jit(solution)/shard_map/dot_general | solution.py:69
  59.3 11.6 %fusion.10 = f32[160,3584]{1,0:T(8,128)} fusion(bf16[160,2048]{1,0:T(8,128)(2,1)S(1)} %all_gather.19, bf16[1,3584,2048]{2,1,0:T(8,128)(2,1)} %param.19), kind=kOutput, calls=%fused_computation.10 | convolution fusion | flops 2348810240 | bytes 17629184 | tf_op jit(solution)/shard_map/dot_general | solution.py:75
  70.9 12.1 %fusion = f32[160,2048]{1,0:T(8,128)S(1)} fusion(bf16[1,2048,3584]{2,1,0:T(8,128)(2,1)} %param.17, f32[160,3584]{1,0:T(8,128)} %fusion.2, f32[160,3584]{1,0:T(8,128)} %fusion.10, f32[160,3584]{1,0:T(8,128)} %fusion.6), kind=kOutput, calls=%fused_computation | convolution fusion | flops 2354544640 | bytes 22872064 | tf_op jit(solution)/shard_map/dot_general | solution.py:78
  83.1 12.8 %fusion.15 = f32[160,2048]{1,0:T(8,128)} fusion(f32[160,2048]{1,0:T(8,128)S(1)} %fusion, bf16[1,2048,3584]{2,1,0:T(8,128)(2,1)} %param.18, f32[160,3584]{1,0:T(8,128)} %fusion.10, f32[160,3584]{1,0:T(8,128)} %fusion.2), kind=kOutput, calls=%fused_computation.13 | convolution fusion | flops 2352578560 | bytes 21889024 | tf_op jit(solution)/shard_map/dot_general | solution.py:78
  95.8 2.2 %reshape.181 = f32[2,80,4,512]{3,2,1,0:T(4,128)S(1)} reshape(f32[160,2048]{1,0:T(8,128)} %fusion.15) | data formatting | bytes 2621440 | tf_op jit(solution)/shard_map/reshape | solution.py:161
  98.0 1.5 multiply_bitcast_fusion
  99.5 0.0 copy-start.12
  99.5 0.0 copy-start.13
  99.6 0.0 copy-start.3
  99.6 0.0 copy-start.4
  99.6 1.6 copy.37
  101.2 0.0 reduce-scatter.2.cloned.1.call-update
  101.2 0.0 all-reduce.5.cloned.1.call-start
  101.3 0.2 reduce-window.17
  101.4 0.6 dynamic-slice.2
  102.7 0.2 fusion.38
  102.9 15.3 %psum.35 = f32[128,64]{0,1:T(8,128)S(1)} all-reduce(f32[128,64]{0,1:T(8,128)S(1)} %fusion.38), channel_id=1, replica_groups=mesh['section'=4,'expert'=4,'dp'=2] {'expert'}, use_global_device_ids=true, to_apply=%region_10.11 | all-reduce | flops 8192 | bytes 65536 | tf_op jit(solution)/shard_map/psum | solution.py:132
  118.2 10.2 %all-gather.1 = bf16[1,2048,64]{1,2,0:T(8,128)(2,1)} all-gather(bf16[1,512,64]{1,2,0:T(8,128)(2,1)S(1)} %copy-done.4), channel_id=3, replica_groups=mesh['section'=4,'expert'=4,'dp'=2] {'expert'}, dimensions={1}, use_global_device_ids=true | all-gather | bytes 327680 | tf_op jit(solution)/shard_map/all_gather | solution.py:130
  128.4 0.1 convert_reduce_fusion
  128.5 10.1 %fusion.20 = f32[160]{0:T(256)} fusion(bf16[1,3584,2048]{2,1,0:T(8,128)(2,1)} %param.19, bf16[160,2048]{1,0:T(8,128)(2,1)S(1)} %all_gather.19, f32[160,3584]{1,0:T(8,128)} %fusion.6, f32[160,3584]{1,0:T(8,128)} %fusion.2), kind=kOutput, calls=%fused_computation.23 | convolution fusion | flops 2353233664 | bytes 19923584 | tf_op jit(solution)/shard_map/dot_general | solution.py:73
  138.6 2.6 %all-reduce = f32[160]{0:T(256)S(1)} all-reduce(f32[160]{0:T(256)} %fusion.20), channel_id=5, replica_groups=mesh['section'=4,'expert'=4,'dp'=2] {'dp'}, use_global_device_ids=true, to_apply=%region_12.13.clone | all-reduce | flops 160 | bytes 1280
  141.2 0.8 convolution_bitcast_fusion.1
  142.1 0.9 convolution_bitcast_fusion
  142.9 2.1 %fusion.30 = f32[1,64,512]{2,1,0:T(8,128)} fusion(bf16[128,2048]{1,0:T(8,128)(2,1)S(1)} %multiply_convert_fusion.7, bf16[1,2048,64]{1,2,0:T(8,128)(2,1)} %all-gather.1, bf16[1,128,512]{2,1,0:T(8,128)(2,1)S(1)} %copy-done.3, s32[128]{0:T(128)S(1)} %convert_reduce_fusion, s32[64]{0:T(128)S(1)} %and_select_fusion), kind=kOutput, calls=%fused_computation.35 | convolution fusion | flops 42000384 | bytes 1049344 | tf_op jit(solution)/shard_map/dot_general | solution.py:137
  145.0 0.7 broadcast_multiply_fusion
  145.7 0.0 all-reduce.5.cloned.1.call-update
  145.7 0.0 reduce-scatter.2.cloned.1.call-done
  145.7 1.4 multiply_reduce_fusion.1
  147.1 8.9 %all-reduce.1 = (f32[128,1]{0,1:T(1,128)S(1)}, f32[128,4]{0,1:T(4,128)S(1)}) all-reduce(f32[128,1]{0,1:T(1,128)S(1)} %bitcast.130, f32[128,4]{0,1:T(4,128)S(1)} %broadcast_multiply_fusion), channel_id=1, replica_groups=mesh['section'=4,'expert'=4,'dp'=2] {'expert'}, use_global_device_ids=true, to_apply=%region_17.18 | all-reduce | flops 640 | bytes 5120 | tf_op jit(solution)/shard_map/psum | solution.py:178
  156.1 0.5 fusion.32
  156.5 0.4 fusion.28
  156.9 3.7 %collective-permute-start = (bf16[128,512]{1,0:T(8,128)(2,1)S(1)}, bf16[128,512]{1,0:T(8,128)(2,1)S(1)}, u32[]{:S(2)}, u32[]{:S(2)}) collective-permute-start(bf16[128,512]{1,0:T(8,128)(2,1)S(1)} %fusion.28), channel_id=1, source_target_pairs={{8,0},{16,8},{24,16},{0,24},{9,1},{17,9},{25,17},{1,25},{10,2},{18... | collective-permute-start | bytes 393224 | tf_op jit(solution)/shard_map/ppermute | solution.py:25
  160.6 2.5 %collective-permute-done = bf16[128,512]{1,0:T(8,128)(2,1)S(1)} collective-permute-done((bf16[128,512]{1,0:T(8,128)(2,1)S(1)}, bf16[128,512]{1,0:T(8,128)(2,1)S(1)}, u32[]{:S(2)}, u32[]{:S(2)}) %collective-permute-start) | collective-permute-done | bytes 131104 | tf_op jit(solution)/shard_map/ppermute | solution.py:25
  163.2 0.9 all-reduce.5.cloned.1.call-done
  164.1 0.7 copy.45
  164.7 1.6 copy.46
  166.3 1.6 copy.47
  (49 shorter events, 0.2 us)
Async XLA Ops:
  8.0 94.7 %copy-start = (bf16[1,64,512]{2,1,0:T(8,128)(2,1)S(1)}, bf16[1,64,512]{2,1,0:T(8,128)(2,1)}, u32[]{:S(2)}) copy-start(bf16[1,64,512]{2,1,0:T(8,128)(2,1)} %param.21) | copy-start | bytes 196612
  8.0 21.1 %copy-start.11 = (s32[1,128,2]{1,2,0:T(2,128)S(1)}, s32[1,128,2]{1,2,0:T(2,128)}, u32[]{:S(2)}) copy-start(s32[1,128,2]{1,2,0:T(2,128)} %param.13) | copy-start | bytes 3076
  9.8 19.3 %all-to-all-start = ((bf16[4,128,512]{2,1,0:T(8,128)(2,1)}), bf16[4,128,512]{2,1,0:T(8,128)(2,1)S(1)}, u32[]{:S(2)}, u32[]{:S(2)}) async-start(bf16[4,128,512]{2,1,0:T(8,128)(2,1)} %stack.3), calls=%async_computation | async-start | bytes 1048576 | tf_op jit(solution)/shard_map/all_to_all | solution.py:19
  15.0 130.7 %reduce-scatter.2.cloned.1.call-start = ((), (), s32[]{:S(2)}) async-start(), calls=%async_computation.2 | async-start | bytes 2359296 | tf_op jit(solution)/shard_map/reduce_scatter | solution.py:164
  29.1 3.3 %copy-start.7 = (f32[4]{0:T(128)}, f32[4]{0:T(128)S(1)}, u32[]{:S(2)}) copy-start(f32[4]{0:T(128)S(1)} %compare_convert_fusion) | copy-start | bytes 52
  29.4 2.7 %copy-start.5 = (bf16[1,2048,4]{1,2,0:T(4,128)(2,1)S(1)}, bf16[1,2048,4]{1,2,0:T(4,128)(2,1)}, u32[]{:S(2)}) copy-start(bf16[1,2048,4]{1,2,0:T(4,128)(2,1)} %param.16) | copy-start | bytes 49156
  30.7 8.6 %copy-start.6 = (f32[1,2048]{1,0:T(1,128)S(1)}, f32[1,2048]{1,0:T(1,128)}, u32[]{:S(2)}) copy-start(f32[1,2048]{1,0:T(1,128)} %param.15) | copy-start | bytes 24580
  30.7 24.6 %slice-start = ((s8[14680064]{0:T(1024)(128)(4,1)}), s8[2097152]{0:T(1024)(128)(4,1)S(1)}, s32[]{:S(2)}) async-start(s8[14680064]{0:T(1024)(128)(4,1)} %bitcast.116), calls=%async_computation.4 | async-start | bytes 4194304
  32.4 8.5 %copy-start.8 = (pred[128]{0:T(512)(128)(4,1)}, pred[128]{0:T(512)(128)(4,1)S(1)}, u32[]{:S(2)}) copy-start(pred[128]{0:T(512)(128)(4,1)S(1)} %convert_compare_fusion) | copy-start | bytes 388
  39.3 1.7 copy-start.10
  41.0 14.4 %slice-start.1 = ((s8[14680064]{0:T(1024)(128)(4,1)}), s8[4194304]{0:T(1024)(128)(4,1)S(1)}, s32[]{:S(2)}) async-start(s8[14680064]{0:T(1024)(128)(4,1)} %bitcast.116), calls=%async_computation.5 | async-start | bytes 8388608
  46.1 9.3 %slice-start.2 = ((s8[14680064]{0:T(1024)(128)(4,1)}), s8[4194304]{0:T(1024)(128)(4,1)S(1)}, s32[]{:S(2)}) async-start(s8[14680064]{0:T(1024)(128)(4,1)} %bitcast.116), calls=%async_computation.6 | async-start | bytes 8388608
  46.1 9.3 %slice-start.3 = ((s8[14680064]{0:T(1024)(128)(4,1)}), s8[4194304]{0:T(1024)(128)(4,1)S(1)}, s32[]{:S(2)}) async-start(s8[14680064]{0:T(1024)(128)(4,1)} %bitcast.116), calls=%async_computation.7 | async-start | bytes 8388608
  99.5 1.7 copy-start.12
  99.5 1.9 %copy-start.13 = (u32[32]{0:T(128)S(1)}, u32[32]{0:T(128)}, u32[]{:S(2)}) copy-start(u32[32]{0:T(128)} %constant.93) | copy-start | bytes 388
  99.6 3.1 %copy-start.3 = (bf16[1,128,512]{2,1,0:T(8,128)(2,1)S(1)}, bf16[1,128,512]{2,1,0:T(8,128)(2,1)}, u32[]{:S(2)}) copy-start(bf16[1,128,512]{2,1,0:T(8,128)(2,1)} %param.12) | copy-start | bytes 393220
  99.6 18.6 %copy-start.4 = (bf16[1,512,64]{1,2,0:T(8,128)(2,1)S(1)}, bf16[1,512,64]{1,2,0:T(8,128)(2,1)}, u32[]{:S(2)}) copy-start(bf16[1,512,64]{1,2,0:T(8,128)(2,1)} %param.20) | copy-start | bytes 196612
  101.2 62.9 %all-reduce.5.cloned.1.call-start = ((), (), s32[]{:S(2)}) async-start(), calls=%async_computation.3 | async-start | bytes 524288 | tf_op jit(solution)/shard_map/psum | solution.py:143
  128.5 12.7 %copy-start.9 = (pred[128]{0:T(512)(128)(4,1)S(1)}, pred[128]{0:T(512)(128)(4,1)}, u32[]{:S(2)}) copy-start(pred[128]{0:T(512)(128)(4,1)} %copy-done.8) | copy-start | bytes 388
  128.5 17.2 %copy-start.1 = (f32[128,2048]{1,0:T(8,128)S(1)}, f32[128,2048]{1,0:T(8,128)}, u32[]{:S(2)}) copy-start(f32[128,2048]{1,0:T(8,128)} %copy.39) | copy-start | bytes 3145732
  138.6 17.4 %copy-start.2 = (f32[4,128,512]{1,2,0:T(8,128)S(1)}, f32[4,128,512]{1,2,0:T(8,128)}, u32[]{:S(2)}) copy-start(f32[4,128,512]{1,2,0:T(8,128)} %get-tuple-element.15) | copy-start | bytes 3145732
  156.9 6.2 %collective-permute-start = (bf16[128,512]{1,0:T(8,128)(2,1)S(1)}, bf16[128,512]{1,0:T(8,128)(2,1)S(1)}, u32[]{:S(2)}, u32[]{:S(2)}) collective-permute-start(bf16[128,512]{1,0:T(8,128)(2,1)S(1)} %fusion.28), channel_id=1, source_target_pairs={{8,0},{16,8},{24,16},{0,24},{9,1},{17,9},{25,17},{1,25},{10,2},{18... | collective-permute-start | bytes 393224 | tf_op jit(solution)/shard_map/ppermute | solution.py:25
Sparse Core Ops, SparseCore 0:
  101.3 42.1 reduce-scatter.1
Sparse Core Ops, SparseCore 1:
  145.8 18.2 all-reduce.4
